TPU v7x, 32 devices: a whole 2x2x4 slice. The times are simulated.
32 devices in a mesh: comp: 2 (over core), dom: 16 (over z, y, x).
Axes of the slice: x: 2, y: 2, z: 4, core: 2. Of those that a mesh axis runs over, the one named last changes fastest.
Arguments:
- surface_flux: float32 [6, 12, 131072], P(None, None, ('comp', 'dom')), may hold values from -8 to 8
- active_mask: int32 [131072], P(('comp', 'dom')), may hold values 0 or 1
- source_area: float32 [131072], P(('comp', 'dom')), may hold values from 0.5 to 30
- tile_targets: int32 [2048, 2], P(('comp', 'dom')), may hold values from 0 to 31, all different within a row
- remap_tiles: float32 [2048, 2, 64, 384], P(('comp', 'dom')), may hold values from -0.0625 to 0.0625
- ocean_flux: float32 [12, 12288], P(None, ('comp', 'dom')), may hold values from -6 to 6
- air_fraction: float32 [3, 12288], P(None, ('comp', 'dom')), may hold values from 0 to 1, as said below
- air_area: float32 [12288], P(('comp', 'dom')), may hold values from 0.5 to 30
Outputs:
- merged: float32 [12, 12288], P(None, ('comp', 'dom'))
- area_means: float32 [3, 12], replicated
Inputs may be any that keep to these rules, and one draw needn't show every extreme that they name: `air_fraction`: the three fractions of a cell are positive and sum to one. `tile_targets`: the 2 targets of one source block differ.
All inputs are finite; a program needn't handle non-finite values. No bound on the sum of `active_mask` on one device may be relied on, other than what follows from the above.
Results may differ from a plain program's by a relative error of at most 0.000071.
Values sent between devices are 32-bit elements; how exact they have to be, the bound alone decides.
A program may use at most 64 MiB of HBM per device.

v0:
```python
import functools

import jax
import jax.numpy as jnp
from jax import lax
from jax.experimental import pallas as pl
from jax.experimental.pallas import tpu as pltpu
from jax.sharding import PartitionSpec as P

MESH = pl.DeviceIdType.MESH
F32 = jnp.float32
BF16 = jnp.bfloat16
CHUNKS = 8
DEPTH = 4
UNROLL = 4


def split(x):
    hi = x.astype(BF16)
    lo = (x - hi.astype(F32)).astype(BF16)
    return hi, lo


def kernel(
    groups,
    domains,
    flux_hbm,
    mask_ref,
    area_ref,
    targets_ref,
    tiles_hbm,
    ocean_ref,
    fraction_ref,
    air_ref,
    merged_ref,
    means_ref,
    flux,
    tiles,
    weighted,
    contrib,
    picks,
    rows_out,
    rows_own,
    rows_in,
    summed,
    partner_in,
    outgoing_a,
    outgoing_b,
    incoming_a,
    incoming_b,
    air_rows,
    stat_out,
    stat_other,
    stat_sum,
    stat_in,
    flux_sem,
    tile_sem,
    row_pair_send,
    row_pair_recv,
    row_send,
    row_recv,
    stat_pair_send,
    stat_pair_recv,
    stat_send,
    stat_recv,
    pair_send,
    pair_recv,
    main_send,
    main_recv,
):
    steps, fields, cells = flux.shape
    blocks, slots, block_cells, air_cells = tiles.shape
    owners = groups * domains
    per_chunk = blocks // CHUNKS
    lane_tiles = air_cells // 128
    tile_count = blocks * slots
    comp = lax.axis_index("comp")
    dom = lax.axis_index("dom")
    other = 1 - comp
    outgoing = (outgoing_a, outgoing_b)
    incoming = (incoming_a, incoming_b)

    flux_copy = pltpu.make_async_copy(flux_hbm, flux, flux_sem)
    flux_copy.start()
    tile_copies = []
    for i in range(CHUNKS):
        part = pl.ds(i * per_chunk, per_chunk)
        copy = pltpu.make_async_copy(tiles_hbm.at[part], tiles.at[part], tile_sem.at[i])
        if i < DEPTH:
            copy.start()
        tile_copies.append(copy)

    barrier = pltpu.get_barrier_semaphore()

    def peer(k):
        p = dom + jnp.where(comp == 0, k, domains - k)
        return jnp.where(p >= domains, p - domains, p)

    peers = list(range(1, domains))
    pl.semaphore_signal(barrier, inc=1, device_id=(other, dom), device_id_type=MESH)
    for k in peers:
        pl.semaphore_signal(barrier, inc=1, device_id=(comp, peer(k)), device_id_type=MESH)

    air = air_ref[...].reshape(1, air_cells)
    for c in range(groups):
        rows_out[c, :, pl.ds(0, air_cells)] = fraction_ref[pl.ds(c, 1), :]
        rows_out[c, :, pl.ds(air_cells, air_cells)] = air
    rows_own[comp] = rows_out[comp]

    row_pair = pltpu.make_async_remote_copy(
        src_ref=rows_out.at[other],
        dst_ref=rows_own.at[comp],
        send_sem=row_pair_send,
        recv_sem=row_pair_recv,
        device_id=(other, dom),
        device_id_type=MESH,
    )

    def row_copy(k, slot):
        return pltpu.make_async_remote_copy(
            src_ref=rows_own,
            dst_ref=rows_in.at[:, slot],
            send_sem=row_send.at[k],
            recv_sem=row_recv.at[slot],
            device_id=(comp, peer(k)),
            device_id_type=MESH,
        )

    pl.semaphore_wait(barrier, domains)
    row_pair.start()
    row_pair.wait()
    for k in peers:
        row_copy(k, dom).start()
    flux_copy.wait()
    weighted[pl.ds(8, 8), :] = jnp.zeros((8, cells), F32)
    width = 512

    def weigh(i, carry):
        total, area_total = carry
        part = pl.ds(pl.multiple_of(i * width, width), width)
        value = flux[0, :, part]
        for s in range(1, steps):
            value = value + flux[s, :, part]
        area = area_ref[:, part]
        value = (value / steps) * (mask_ref[:, part].astype(F32) * area)
        weighted[pl.ds(0, fields), part] = value
        return total + value, area_total + area

    total, area_total = lax.fori_loop(
        0,
        cells // width,
        weigh,
        (jnp.zeros((fields, width), F32), jnp.zeros((1, width), F32)),
        unroll=2,
    )
    surface_num = jnp.sum(total, axis=1, keepdims=True)
    surface_den = jnp.sum(area_total)

    lane = lax.broadcasted_iota(jnp.int32, (16, 128), 1)
    first = lane < block_cells
    blank = jnp.zeros((16, 128), BF16)

    def pair(j, carry):
        cell = pl.ds(pl.multiple_of(j * 128, 128), 128)
        w = weighted[:, cell]
        lhs = []
        for keep in (first, ~first):
            hi, lo = split(jnp.where(keep, w, 0.0))
            lhs.append(jnp.concatenate([hi, hi], axis=1))
            lhs.append(jnp.concatenate([lo, blank], axis=1))
        left = jnp.concatenate(lhs, axis=0)
        for t in range(slots):
            weights = tiles[pl.ds(2 * j, 2), t].reshape(2 * block_cells, air_cells)
            hi, lo = split(weights)
            right = jnp.concatenate([hi, lo], axis=0)
            r = jnp.dot(left, right, preferred_element_type=F32)
            even = r[0:16] + r[16:32]
            odd = r[32:48] + r[48:64]
            base = pl.multiple_of((t * blocks + 2 * j) * 16, 32)
            for q in range(lane_tiles):
                cut = slice(q * 128, (q + 1) * 128)
                contrib[q, pl.ds(base, 16), :] = even[:, cut]
                contrib[q, pl.ds(base + 16, 16), :] = odd[:, cut]
        return carry

    pairs = per_chunk // 2
    for i in range(CHUNKS):
        tile_copies[i].wait()
        if i + DEPTH < CHUNKS:
            tile_copies[i + DEPTH].start()
        lax.fori_loop(i * pairs, (i + 1) * pairs, pair, 0, unroll=UNROLL)

    picks[:, pl.ds(0, blocks)] = targets_ref[...]
    picks[:, pl.ds(blocks, blocks)] = targets_ref[...]
    picked = jnp.where(
        lax.broadcasted_iota(jnp.int32, (1, tile_count), 1) < blocks,
        picks[pl.ds(0, 1), :],
        picks[pl.ds(1, 1), :],
    )
    owner_ids = lax.broadcasted_iota(jnp.int32, (owners, tile_count), 0)
    selector = jnp.where(owner_ids == picked, 1.0, 0.0).astype(BF16)
    selector = jnp.concatenate([selector, selector], axis=1)

    air_rows[...] = jnp.zeros(air_rows.shape, F32)

    def collect(f, carry):
        right = []
        for q in range(lane_tiles):
            hi, lo = split(contrib[q, pl.ds(f, tile_count, stride=16), :])
            right.append(jnp.concatenate([hi, lo], axis=0))
        s = jnp.dot(selector, jnp.concatenate(right, axis=1), preferred_element_type=F32)
        summed[f] = s
        return carry

    lax.fori_loop(0, 8, collect, 0, unroll=4)

    rows_in[:, pl.ds(dom, 1)] = rows_own[...].reshape(groups, 1, 1, 2 * air_cells)
    for k in peers:
        row_copy(k, peer(k)).wait_recv()

    rows = rows_in[...].reshape(owners, 2 * air_cells)
    fraction = rows[:, :air_cells]
    scale = fraction / rows[:, air_cells:]

    def weigh_sums(f, carry):
        s = summed[f]
        summed[f] = s * scale
        air_rows[pl.ds(f, 1), :] = jnp.sum(s * fraction, axis=0, keepdims=True)
        return carry

    far = pl.ds(pl.multiple_of(other * domains, 8), domains)
    cuts = [(0, 8), (8, fields - 8)]
    pair_copies = []
    for n, (low, count) in enumerate(cuts):
        if n > 0:
            lax.fori_loop(low, low + count, collect, 0, unroll=4)
        lax.fori_loop(low, low + count, weigh_sums, 0, unroll=4)
        part = pl.ds(low, count)
        copy = pltpu.make_async_remote_copy(
            src_ref=summed.at[part, far],
            dst_ref=partner_in.at[part],
            send_sem=pair_send.at[n],
            recv_sem=pair_recv.at[n],
            device_id=(other, dom),
            device_id_type=MESH,
        )
        copy.start()
        pair_copies.append(copy)
    ocean = fraction_ref[pl.ds(2, 1), :] * ocean_ref[...]
    air_num = jnp.sum(air_rows[pl.ds(0, fields), :] + air * ocean, axis=1, keepdims=True)
    air_den = jnp.sum(air)
    spot = lax.broadcasted_iota(jnp.int32, (fields, 128), 1)
    line = lax.broadcasted_iota(jnp.int32, (fields, 128), 0)
    stat = jnp.where(spot == line + 16 * comp, surface_num, 0.0)
    stat = stat + jnp.where(spot == line + 16 * groups, air_num, 0.0)
    stat = jnp.sum(stat, axis=0, keepdims=True)
    spot = lax.broadcasted_iota(jnp.int32, (1, 128), 1)
    dens = 16 * (groups + 1)
    stat = stat + jnp.where(spot == dens + comp, surface_den, 0.0)
    stat = stat + jnp.where(spot == dens + groups, air_den, 0.0)
    stat_out[...] = stat
    stat_pair = pltpu.make_async_remote_copy(
        src_ref=stat_out,
        dst_ref=stat_other,
        send_sem=stat_pair_send,
        recv_sem=stat_pair_recv,
        device_id=(other, dom),
        device_id_type=MESH,
    )
    stat_pair.start()

    def stat_copy(k, slot):
        return pltpu.make_async_remote_copy(
            src_ref=stat_sum,
            dst_ref=stat_in.at[slot],
            send_sem=stat_send.at[k],
            recv_sem=stat_recv.at[slot],
            device_id=(comp, peer(k)),
            device_id_type=MESH,
        )

    own = pl.ds(pl.multiple_of(comp * domains, 8), domains)

    def main_copy(n, k, slot):
        p = peer(k)
        return pltpu.make_async_remote_copy(
            src_ref=outgoing[n].at[p],
            dst_ref=incoming[n].at[slot],
            send_sem=main_send.at[n, k],
            recv_sem=main_recv.at[n, slot],
            device_id=(comp, p),
            device_id_type=MESH,
        )

    def send_group(n):
        low, count = cuts[n]
        pair_copies[n].wait()
        for f in range(low, low + count):
            outgoing[n][:, f - low, :] = summed[f, own, :] + partner_in[f]
        for k in peers:
            main_copy(n, k, dom).start()

    send_group(0)
    stat_pair.wait()
    stat = stat_out[...] + stat_other[...]
    stat_sum[...] = stat
    stat_in[dom] = stat
    for k in peers:
        stat_copy(k, dom).start()
    send_group(1)

    for n, (low, count) in enumerate(cuts):
        merged_ref[pl.ds(low, count), :] = ocean[low : low + count] + outgoing[n][dom]

    for n, (low, count) in enumerate(cuts):
        part = pl.ds(low, count)
        total = merged_ref[part, :]
        for k in peers:
            slot = peer(k)
            main_copy(n, k, slot).wait_recv()
            total = total + incoming[n][slot]
        merged_ref[part, :] = total
    for k in peers:
        stat_copy(k, peer(k)).wait_recv()

    stat = jnp.sum(stat_in[...], axis=0)
    for c in range(groups + 1):
        den = jnp.sum(jnp.where(spot == dens + c, stat, 0.0))
        moved = stat if c == 0 else pltpu.roll(stat, 128 - 16 * c, 1)
        means_ref[pl.ds(c, 1), :] = moved[:, :fields] / den

    for k in peers:
        row_copy(k, dom).wait_send()
        main_copy(0, k, dom).wait_send()
        main_copy(1, k, dom).wait_send()
        stat_copy(k, dom).wait_send()


def finish(merged_in, means_in, merged_ref, means_ref):
    merged_ref[...] = merged_in[...]
    means_ref[...] = means_in[...]


def on_device(
    surface_flux,
    active_mask,
    source_area,
    tile_targets,
    remap_tiles,
    ocean_flux,
    air_fraction,
    air_area,
):
    groups = lax.axis_size("comp")
    domains = lax.axis_size("dom")
    owners = groups * domains
    fields = surface_flux.shape[1]
    cells = surface_flux.shape[2]
    blocks, slots, block_cells, air_cells = remap_tiles.shape
    vmem = pl.BlockSpec(memory_space=pltpu.VMEM)
    hbm = pl.BlockSpec(memory_space=pl.ANY)
    dma = pltpu.SemaphoreType.DMA
    shapes = (
        jax.ShapeDtypeStruct((fields, air_cells), F32),
        jax.ShapeDtypeStruct((groups + 1, fields), F32),
    )
    parts = pl.pallas_call(
        functools.partial(kernel, groups, domains),
        out_shape=shapes,
        in_specs=[hbm, vmem, vmem, vmem, hbm, vmem, vmem, vmem],
        out_specs=(vmem, vmem),
        scratch_shapes=[
            pltpu.VMEM(surface_flux.shape, F32),
            pltpu.VMEM(remap_tiles.shape, F32),
            pltpu.VMEM((16, cells), F32),
            pltpu.VMEM((air_cells // 128, blocks * slots * 16, 128), F32),
            pltpu.VMEM((slots, blocks * slots), jnp.int32),
            pltpu.VMEM((groups, 1, 2 * air_cells), F32),
            pltpu.VMEM((groups, 1, 2 * air_cells), F32),
            pltpu.VMEM((groups, domains, 1, 2 * air_cells), F32),
            pltpu.VMEM((fields, owners, air_cells), F32),
            pltpu.VMEM((fields, domains, air_cells), F32),
            pltpu.VMEM((domains, 8, air_cells), F32),
            pltpu.VMEM((domains, fields - 8, air_cells), F32),
            pltpu.VMEM((domains, 8, air_cells), F32),
            pltpu.VMEM((domains, fields - 8, air_cells), F32),
            pltpu.VMEM((16, air_cells), F32),
            pltpu.VMEM((1, 128), F32),
            pltpu.VMEM((1, 128), F32),
            pltpu.VMEM((1, 128), F32),
            pltpu.VMEM((domains, 1, 128), F32),
            dma,
            dma((CHUNKS,)),
            dma,
            dma,
            dma((domains,)),
            dma((domains,)),
            dma,
            dma,
            dma((domains,)),
            dma((domains,)),
            dma((2,)),
            dma((2,)),
            dma((2, domains)),
            dma((2, domains)),
        ],
        compiler_params=pltpu.CompilerParams(
            collective_id=0, has_side_effects=True, vmem_limit_bytes=60 * 1024 * 1024
        ),
    )(
        surface_flux,
        active_mask.reshape(1, cells),
        source_area.reshape(1, cells),
        tile_targets.T,
        remap_tiles,
        ocean_flux,
        air_fraction,
        air_area,
    )
    return pl.pallas_call(
        finish, out_shape=shapes, in_specs=[vmem, vmem], out_specs=(vmem, vmem)
    )(*parts)


def solution(mesh):
    in_specs = (
        P(None, None, ("comp", "dom")),
        P(("comp", "dom")),
        P(("comp", "dom")),
        P(("comp", "dom"), None),
        P(("comp", "dom"), None, None, None),
        P(None, ("comp", "dom")),
        P(None, ("comp", "dom")),
        P(("comp", "dom")),
    )
    out_specs = (P(None, ("comp", "dom")), P())
    return jax.shard_map(
        on_device, mesh=mesh, in_specs=in_specs, out_specs=out_specs, check_vma=False
    )
```

profile of v0, /device:TPU:1, one launch (start us, length us, event | category | flops | bytes accessed | tf_op | source)
XLA Modules:
  0.0 28.0 jit_solution(14936957993479926506)
XLA Ops:
  0.6 26.0 %shard_map.95 = (f32[12,384]{1,0:T(8,128)}, f32[3,12]{1,0:T(4,128)}) custom-call(f32[6,12,4096]{2,1,0:T(8,128)} %flux_hbm.1, s32[1,4096]{1,0:T(1,128)} %bitcast.3, f32[1,4096]{1,0:T(1,128)} %bitcast.4, s32[2,64]{1,0:T(2,128)} %bitcast.5, f32[64,2,64,384]{3,2,1,0:T(8,128)} %tiles_hbm.1, f32[12,384]{1,0:T(8,128)} %ocean_ref.1, f32[3,384]{1,0:T(4,128)} %fraction_ref.1, ...), custom_call_target="tpu_custom_call" | custom-call | tf_op jit(solution)/shard_map/pallas_call | solution.py:367
  26.7 1.4 %shard_map.96 = (f32[12,384]{1,0:T(8,128)}, f32[3,12]{1,0:T(4,128)}) custom-call(f32[12,384]{1,0:T(8,128)} %get-tuple-element.4.merged_in, f32[3,12]{1,0:T(4,128)} %get-tuple-element.5.means_in), custom_call_target="tpu_custom_call" | custom-call | tf_op jit(solution)/shard_map/pallas_call | solution.py:420
where the time goes:
time: 28.3 us; the launch traced here: 28 us
  Pallas kernels  27.4 us (97%)
  between operations  0.64 us (2%)
    pallas_call x1, Pallas kernels, on_device(): pl.pallas_call(functools.partial(kernel, groups, domains), out_shape=shap...  26 us
    pallas_call x1, Pallas kernels, on_device(): pl.pallas_call(finish, out_shape=shapes, in_specs=[vmem, vmem], out_specs...  1.35 us

commit v1 on v0

v1 whole, which is shorter than its diff:
```python
import functools

import jax
import jax.numpy as jnp
from jax import lax
from jax.experimental import pallas as pl
from jax.experimental.pallas import tpu as pltpu
from jax.sharding import PartitionSpec as P

MESH = pl.DeviceIdType.MESH
F32 = jnp.float32
BF16 = jnp.bfloat16
AHEAD = 2
SEND_ROWS_AT = 4
FLUX_PARTS = 4
UNROLL = 4
PAIR_CUTS = 3


def split(x):
    hi = x.astype(BF16)
    lo = (x - hi.astype(F32)).astype(BF16)
    return hi, lo


def chunk_sizes(blocks):
    whole = blocks // 8
    return [whole] * 7 + [whole // 2] * 2


def kernel(
    groups,
    domains,
    flux_hbm,
    mask_hbm,
    area_hbm,
    targets_hbm,
    tiles_hbm,
    ocean_hbm,
    fraction_hbm,
    air_hbm,
    merged_ref,
    means_ref,
    flux,
    mask,
    area,
    targets,
    tiles,
    ocean,
    fraction,
    air,
    stacked,
    lhs,
    contrib,
    picks,
    row_out,
    rows_in,
    summed,
    air_parts,
    partner_in,
    stat_out,
    stat_in,
    outgoing,
    incoming,
    flux_sem,
    tile_sem,
    small_sem,
    row_send,
    row_recv,
    pair_send,
    pair_recv,
    stat_send,
    stat_recv,
    main_send,
    main_recv,
):
    steps, fields, cells = flux.shape
    blocks, slots, block_cells, air_cells = tiles.shape
    owners = groups * domains
    chunks = chunk_sizes(blocks)
    lane_tiles = air_cells // 128
    tile_count = blocks * slots
    body_rows = lane_tiles * fields
    comp = lax.axis_index("comp")
    dom = lax.axis_index("dom")
    other = 1 - comp

    small = [
        pltpu.make_async_copy(src, dst, small_sem.at[i])
        for i, (src, dst) in enumerate(
            [
                (fraction_hbm, fraction),
                (mask_hbm, mask),
                (area_hbm, area),
                (targets_hbm, targets),
                (ocean_hbm, ocean),
                (air_hbm, air),
            ]
        )
    ]
    for copy in small[:3]:
        copy.start()
    flux_width = cells // FLUX_PARTS
    flux_copies = []
    for i in range(FLUX_PARTS):
        part = pl.ds(i * flux_width, flux_width)
        copy = pltpu.make_async_copy(
            flux_hbm.at[:, :, part], flux.at[:, :, part], flux_sem.at[i]
        )
        copy.start()
        flux_copies.append(copy)
    tile_copies = []
    low = 0
    for i, size in enumerate(chunks):
        part = pl.ds(low, size)
        low += size
        tile_copies.append(
            pltpu.make_async_copy(tiles_hbm.at[part], tiles.at[part], tile_sem.at[i])
        )
    waiting = list(tile_copies)

    def start_more(count):
        for copy in waiting[:count]:
            copy.start()
        del waiting[:count]

    start_more(AHEAD)

    barrier = pltpu.get_barrier_semaphore()
    rivals = []
    for k in range(domains - 1):
        rivals.append((comp, k + jnp.where(dom <= k, 1, 0)))
    mates = [(other, k) for k in range(domains)]
    for a, b in zip(rivals + [None], mates):
        for peer in (a, b):
            if peer is not None:
                pl.semaphore_signal(barrier, inc=1, device_id=peer, device_id_type=MESH)

    small[1].wait()
    small[2].wait()
    width = min(512, flux_width)
    lane = lax.broadcasted_iota(jnp.int32, (fields, width), 1)
    first = lax.rem(lane, 2 * block_cells) < block_cells

    def weigh(i, carry):
        total, area_total = carry
        part = pl.ds(pl.multiple_of(i * width, width), width)
        value = flux[0, :, part]
        for s in range(1, steps):
            value = value + flux[s, :, part]
        a = area[:, part]
        value = (value / steps) * (mask[:, part].astype(F32) * a)
        stacked[pl.ds(0, fields), part] = jnp.where(first, value, 0.0)
        stacked[pl.ds(fields, fields), part] = jnp.where(first, 0.0, value)
        both = stacked[:, part]
        hi = both.astype(BF16).astype(F32)
        left = jnp.concatenate([hi, both - hi], axis=0).astype(BF16)
        right = jnp.concatenate([hi, jnp.zeros_like(hi)], axis=0).astype(BF16)
        for j in range(width // 128):
            cut = slice(j * 128, (j + 1) * 128)
            base = pl.multiple_of(2 * i * width + 256 * j, 256)
            lhs[:, pl.ds(base, 128)] = left[:, cut]
            lhs[:, pl.ds(base + 128, 128)] = right[:, cut]
        return total + value, area_total + a

    carry = (jnp.zeros((fields, width), F32), jnp.zeros((1, width), F32))
    rounds = flux_width // width
    for i in range(FLUX_PARTS):
        flux_copies[i].wait()
        start_more(1)
        carry = lax.fori_loop(i * rounds, (i + 1) * rounds, weigh, carry, unroll=rounds)
    surface_num = jnp.sum(carry[0], axis=1, keepdims=True)
    surface_den = jnp.sum(carry[1])

    def pair(j, carry):
        left = lhs[:, pl.ds(pl.multiple_of(j * 256, 256), 256)]
        right = []
        for t in range(slots):
            weights = tiles[pl.ds(2 * j, 2), t].reshape(2 * block_cells, air_cells)
            hi, lo = split(weights)
            right.append(jnp.concatenate([hi, lo], axis=0))
        r = jnp.dot(left, jnp.concatenate(right, axis=1), preferred_element_type=F32)
        r = r[: 2 * fields] + r[2 * fields :]
        for t in range(slots):
            base = pl.multiple_of((t * blocks + 2 * j) * fields, 2 * fields)
            for q in range(lane_tiles):
                n = t * lane_tiles + q
                contrib[q, pl.ds(base, 2 * fields), :] = r[:, n * 128 : (n + 1) * 128]
        return carry

    def row_copy(p, slot):
        return pltpu.make_async_remote_copy(
            src_ref=row_out,
            dst_ref=rows_in.at[pl.ds(pl.multiple_of(slot * 8, 8), groups * lane_tiles)],
            send_sem=row_send,
            recv_sem=row_recv,
            device_id=(comp, p),
            device_id_type=MESH,
        )

    low = 0
    for i, size in enumerate(chunks):
        if i == SEND_ROWS_AT:
            small[0].wait()
            for c in range(groups):
                for q in range(lane_tiles):
                    row = fraction[pl.ds(c, 1), pl.ds(q * 128, 128)]
                    row_out[pl.ds(c * lane_tiles + q, 1), :] = row
                    rows_in[pl.ds(dom * 8 + c * lane_tiles + q, 1), :] = row
            pl.semaphore_wait(barrier, owners - 1)
            for c, p in rivals:
                row_copy(p, dom).start()
        tile_copies[i].wait()
        start_more(1)
        if i == 3:
            for copy in small[3:]:
                copy.start()
        pairs = size // 2
        lax.fori_loop(low, low + pairs, pair, 0, unroll=min(UNROLL, pairs))
        low += pairs

    small[3].wait()
    picks[:, pl.ds(0, blocks)] = targets[...]
    picks[:, pl.ds(blocks, blocks)] = targets[...]
    picked = jnp.where(
        lax.broadcasted_iota(jnp.int32, (1, tile_count), 1) < blocks,
        picks[pl.ds(0, 1), :],
        picks[pl.ds(1, 1), :],
    )
    owner_ids = lax.broadcasted_iota(jnp.int32, (owners, tile_count), 0)
    selector = jnp.where(owner_ids == picked, 1.0, 0.0).astype(BF16)
    selector = jnp.concatenate([selector, selector], axis=1)

    def collect(g, carry):
        right = []
        for f in (2 * g, 2 * g + 1):
            for q in range(lane_tiles):
                hi, lo = split(contrib[q, pl.ds(f, tile_count, stride=fields), :])
                right.append(jnp.concatenate([hi, lo], axis=0))
        s = jnp.dot(selector, jnp.concatenate(right, axis=1), preferred_element_type=F32)
        for n, f in enumerate((2 * g, 2 * g + 1)):
            summed[f] = s[:, n * air_cells : (n + 1) * air_cells]
        return carry

    far = pl.ds(pl.multiple_of(other * domains, 8), domains)
    own = pl.ds(pl.multiple_of(comp * domains, 8), domains)
    per_cut = fields // PAIR_CUTS
    pair_copies = []
    for n in range(PAIR_CUTS):
        lax.fori_loop(n * per_cut // 2, (n + 1) * per_cut // 2, collect, 0, unroll=per_cut // 2)
        part = pl.ds(n * per_cut, per_cut)
        copy = pltpu.make_async_remote_copy(
            src_ref=summed.at[part, far],
            dst_ref=partner_in.at[part],
            send_sem=pair_send.at[n],
            recv_sem=pair_recv.at[n],
            device_id=(other, dom),
            device_id_type=MESH,
        )
        copy.start()
        pair_copies.append(copy)

    small[4].wait()
    small[5].wait()
    air_row = air[...].reshape(1, air_cells)
    inverse = 1.0 / air_row
    ocean_part = fraction[pl.ds(2, 1), :] * ocean[...]
    wet = air_row * ocean_part
    wet = sum(wet[:, q * 128 : (q + 1) * 128] for q in range(lane_tiles))
    air_den = jnp.sum(air_row)
    spot = lax.broadcasted_iota(jnp.int32, (fields, 128), 1)
    line = lax.broadcasted_iota(jnp.int32, (fields, 128), 0)
    stat = jnp.where(spot == line + 16 * comp, surface_num, 0.0)
    stat = jnp.sum(stat, axis=0, keepdims=True)
    spot1 = lax.broadcasted_iota(jnp.int32, (1, 128), 1)
    lead = spot1 - 64
    stat = stat + jnp.where((lead >= 16 * comp) & (lead < 16 * comp + 16), surface_den, 0.0)
    stat = stat + jnp.where(
        (lead >= 16 * groups) & (lead < 16 * groups + 16), air_den, 0.0
    )

    pltpu.make_async_remote_copy(
        src_ref=rows_in.at[pl.ds(0, (domains - 1) * groups * lane_tiles)],
        dst_ref=rows_in.at[pl.ds(0, (domains - 1) * groups * lane_tiles)],
        send_sem=row_send,
        recv_sem=row_recv,
        device_id=(other, dom),
        device_id_type=MESH,
    ).wait_recv()

    def shares(c):
        return [
            rows_in[pl.ds(c * lane_tiles + q, domains, stride=8), :]
            for q in range(lane_tiles)
        ]

    share_own = shares(comp)
    share_other = shares(other)

    def main_copy(p, slot):
        return pltpu.make_async_remote_copy(
            src_ref=outgoing.at[p, pl.ds(0, body_rows + 1)],
            dst_ref=incoming.at[slot, pl.ds(0, body_rows + 1)],
            send_sem=main_send,
            recv_sem=main_recv.at[slot],
            device_id=(comp, p),
            device_id_type=MESH,
        )

    def stat_copy(p, slot):
        return pltpu.make_async_remote_copy(
            src_ref=stat_out,
            dst_ref=stat_in.at[slot],
            send_sem=stat_send,
            recv_sem=stat_recv,
            device_id=(other, p),
            device_id_type=MESH,
        )

    for n in range(PAIR_CUTS):
        pair_copies[n].wait_recv()
        for f in range(n * per_cut, (n + 1) * per_cut):
            acc = None
            for q in range(lane_tiles):
                cut = pl.ds(q * 128, 128)
                both = share_own[q] * summed[f, own, cut]
                both = both + share_other[q] * partner_in[f, :, cut]
                outgoing[:, q * fields + f, :] = both
                acc = both if acc is None else acc + both
            air_parts[pl.ds(f, 1), :] = jnp.sum(acc, axis=0, keepdims=True)
    air_num = jnp.sum(air_parts[...] + wet, axis=1, keepdims=True)
    air_num = jnp.where(spot == line + 16 * groups, air_num, 0.0)
    stat = stat + jnp.sum(air_num, axis=0, keepdims=True)
    outgoing[:, body_rows, :] = jnp.broadcast_to(stat, (domains, 128))
    stat_out[...] = stat
    for k in range(domains):
        stat_copy(k, dom).start()
    for c, p in rivals:
        main_copy(p, dom).start()

    sums = []
    for q in range(lane_tiles):
        sums.append(outgoing[dom, pl.ds(q * fields, fields), :])
    for c, p in rivals:
        main_copy(p, p).wait_recv()
        for q in range(lane_tiles):
            sums[q] = sums[q] + incoming[p, pl.ds(q * fields, fields), :]
        stat = stat + incoming[p, pl.ds(body_rows, 1), :]
    for q in range(lane_tiles):
        cut = slice(q * 128, (q + 1) * 128)
        merged_ref[:, cut] = sums[q] * inverse[:, cut] + ocean_part[:, cut]

    pltpu.make_async_remote_copy(
        src_ref=stat_in,
        dst_ref=stat_in,
        send_sem=stat_send,
        recv_sem=stat_recv,
        device_id=(other, dom),
        device_id_type=MESH,
    ).wait_recv()
    stat = stat + jnp.sum(stat_in[...], axis=0)
    mean = stat / pltpu.roll(stat, 64, 1)
    for c in range(groups + 1):
        moved = mean if c == 0 else pltpu.roll(mean, 128 - 16 * c, 1)
        means_ref[pl.ds(c, 1), :] = moved[:, :fields]

    pltpu.make_async_remote_copy(
        src_ref=rows_in.at[pl.ds(0, (domains - 1) * groups * lane_tiles)],
        dst_ref=rows_in.at[pl.ds(0, (domains - 1) * groups * lane_tiles)],
        send_sem=row_send,
        recv_sem=row_recv,
        device_id=(other, dom),
        device_id_type=MESH,
    ).wait_send()
    for copy in pair_copies:
        copy.wait_send()
    pltpu.make_async_remote_copy(
        src_ref=stat_in,
        dst_ref=stat_in,
        send_sem=stat_send,
        recv_sem=stat_recv,
        device_id=(other, dom),
        device_id_type=MESH,
    ).wait_send()
    pltpu.make_async_remote_copy(
        src_ref=outgoing.at[pl.ds(0, domains - 1), pl.ds(0, body_rows + 1)],
        dst_ref=outgoing.at[pl.ds(0, domains - 1), pl.ds(0, body_rows + 1)],
        send_sem=main_send,
        recv_sem=main_recv.at[0],
        device_id=(other, dom),
        device_id_type=MESH,
    ).wait_send()


def finish(merged_in, means_in, merged_ref, means_ref):
    merged_ref[...] = merged_in[...]
    means_ref[...] = means_in[...]


def on_device(
    surface_flux,
    active_mask,
    source_area,
    tile_targets,
    remap_tiles,
    ocean_flux,
    air_fraction,
    air_area,
):
    groups = lax.axis_size("comp")
    domains = lax.axis_size("dom")
    owners = groups * domains
    fields = surface_flux.shape[1]
    cells = surface_flux.shape[2]
    blocks, slots, block_cells, air_cells = remap_tiles.shape
    lane_tiles = air_cells // 128
    message = -(-(lane_tiles * fields + 1) // 8) * 8
    vmem = pl.BlockSpec(memory_space=pltpu.VMEM)
    hbm = pl.BlockSpec(memory_space=pltpu.HBM)
    dma = pltpu.SemaphoreType.DMA
    parts = pl.pallas_call(
        functools.partial(kernel, groups, domains),
        out_shape=(
            pltpu.VMEM((fields, air_cells), F32),
            pltpu.VMEM((groups + 1, fields), F32),
        ),
        in_specs=[hbm] * 8,
        out_specs=(vmem, vmem),
        scratch_shapes=[
            pltpu.VMEM(surface_flux.shape, F32),
            pltpu.VMEM((1, cells), jnp.int32),
            pltpu.VMEM((1, cells), F32),
            pltpu.VMEM((slots, blocks), jnp.int32),
            pltpu.VMEM(remap_tiles.shape, F32),
            pltpu.VMEM(ocean_flux.shape, F32),
            pltpu.VMEM(air_fraction.shape, F32),
            pltpu.VMEM((air_cells,), F32),
            pltpu.VMEM((2 * fields, cells), F32),
            pltpu.VMEM((4 * fields, 2 * cells), BF16),
            pltpu.VMEM((lane_tiles, blocks * slots * fields, 128), F32),
            pltpu.VMEM((slots, blocks * slots), jnp.int32),
            pltpu.VMEM((groups * lane_tiles, 128), F32),
            pltpu.VMEM((domains * 8, 128), F32),
            pltpu.VMEM((fields, owners, air_cells), F32),
            pltpu.VMEM((fields, 128), F32),
            pltpu.VMEM((fields, domains, air_cells), F32),
            pltpu.VMEM((1, 128), F32),
            pltpu.VMEM((domains, 1, 128), F32),
            pltpu.VMEM((domains, message, 128), F32),
            pltpu.VMEM((domains, message, 128), F32),
            dma((FLUX_PARTS,)),
            dma((len(chunk_sizes(blocks)),)),
            dma((6,)),
            dma,
            dma,
            dma((PAIR_CUTS,)),
            dma((PAIR_CUTS,)),
            dma,
            dma,
            dma,
            dma((domains,)),
        ],
        compiler_params=pltpu.CompilerParams(
            collective_id=0, has_side_effects=True, vmem_limit_bytes=60 * 1024 * 1024
        ),
    )(
        surface_flux,
        active_mask.reshape(1, cells),
        source_area.reshape(1, cells),
        tile_targets.T,
        remap_tiles,
        ocean_flux,
        air_fraction,
        air_area,
    )
    return pl.pallas_call(
        finish,
        out_shape=(
            jax.ShapeDtypeStruct((fields, air_cells), F32),
            jax.ShapeDtypeStruct((groups + 1, fields), F32),
        ),
        in_specs=[vmem, vmem],
        out_specs=(vmem, vmem),
    )(*[pltpu.with_memory_space_constraint(p, pltpu.VMEM) for p in parts])


def solution(mesh):
    in_specs = (
        P(None, None, ("comp", "dom")),
        P(("comp", "dom")),
        P(("comp", "dom")),
        P(("comp", "dom"), None),
        P(("comp", "dom"), None, None, None),
        P(None, ("comp", "dom")),
        P(None, ("comp", "dom")),
        P(("comp", "dom")),
    )
    out_specs = (P(None, ("comp", "dom")), P())
    return jax.shard_map(
        on_device, mesh=mesh, in_specs=in_specs, out_specs=out_specs, check_vma=False
    )
```

time: 28.3 us -> 21 us (0.74)
  the two profiles are of different devices: /device:TPU:1 before, /device:TPU:0 now
where the time goes in v1:
time: 21 us; the launch traced here: 20.9 us
  Pallas kernels  20.2 us (96%)
  between operations  0.64 us (3%)
    pallas_call x1, Pallas kernels, on_device(): pl.pallas_call(functools.partial(kernel, groups, domains), out_shape=(plt...  19.6 us
    pallas_call x1, Pallas kernels, on_device(): pl.pallas_call(finish, out_shape=(jax.ShapeDtypeStruct((fields, air_cells...  0.61 us

profile of v1, /device:TPU:0, one launch (start us, length us, event | category | flops | bytes accessed | tf_op | source)
XLA Modules:
  0.0 20.9 jit_solution(4628988340701682662)
XLA Ops:
  0.6 19.6 %shard_map.95 = (f32[12,384]{1,0:T(8,128)S(1)}, f32[3,12]{1,0:T(4,128)S(1)}) custom-call(f32[6,12,4096]{2,1,0:T(8,128)} %flux_hbm.1, s32[1,4096]{1,0:T(1,128)} %bitcast.3, f32[1,4096]{1,0:T(1,128)} %bitcast.4, s32[2,64]{1,0:T(2,128)} %bitcast.5, f32[64,2,64,384]{3,2,1,0:T(8,128)} %tiles_hbm.1, f32[12,384]{1,0:T(8,128)} %ocean_hbm.1, f32[3,384]{1,0:T(4,128)} %fraction_hbm.1, ...), custom_call_target="tpu_custom_call" | custom-call | tf_op jit(solution)/shard_map/pallas_call | solution.py:421
  20.3 0.6 %shard_map.96 = (f32[12,384]{1,0:T(8,128)}, f32[3,12]{1,0:T(4,128)}) custom-call(f32[12,384]{1,0:T(8,128)S(1)} %get-tuple-element.4.merged_in, f32[3,12]{1,0:T(4,128)S(1)} %get-tuple-element.5.means_in), custom_call_target="tpu_custom_call" | custom-call | tf_op jit(solution)/shard_map/pallas_call | solution.py:476

commit v2 on v1

--- a/solution.py
+++ b/solution.py
@@ -10,11 +10,14 @@
 MESH = pl.DeviceIdType.MESH
 F32 = jnp.float32
 BF16 = jnp.bfloat16
-AHEAD = 2
-SEND_ROWS_AT = 4
-FLUX_PARTS = 4
-UNROLL = 4
+DEPTH = 8
+EXTRA = 4
+SEND_ROWS_AT = 2
+PARTS = 4
+UNROLL = 8
 PAIR_CUTS = 3
+AT_ONCE = 1
+SIDE_AT = 1
 
 
 def split(x):
@@ -23,9 +26,11 @@
     return hi, lo
 
 
-def chunk_sizes(blocks):
-    whole = blocks // 8
-    return [whole] * 7 + [whole // 2] * 2
+def plan(blocks):
+    whole = blocks // PARTS
+    copies = [[whole // 4] * 4] * PARTS
+    rounds = [[whole // 2] * 2] + [[whole]] * (PARTS - 2) + [[whole // 2, whole // 4, whole // 4]]
+    return copies, rounds
 
 
 def kernel(
@@ -62,6 +67,7 @@
     stat_in,
     outgoing,
     incoming,
+    relayed,
     flux_sem,
     tile_sem,
     small_sem,
@@ -77,9 +83,8 @@
     steps, fields, cells = flux.shape
     blocks, slots, block_cells, air_cells = tiles.shape
     owners = groups * domains
-    chunks = chunk_sizes(blocks)
+    copy_plan, round_plan = plan(blocks)
     lane_tiles = air_cells // 128
-    tile_count = blocks * slots
     body_rows = lane_tiles * fields
     comp = lax.axis_index("comp")
     dom = lax.axis_index("dom")
@@ -98,33 +103,36 @@
             ]
         )
     ]
-    for copy in small[:3]:
+    for copy in small[1:3]:
         copy.start()
-    flux_width = cells // FLUX_PARTS
+    flux_width = cells // PARTS
     flux_copies = []
-    for i in range(FLUX_PARTS):
+    tile_copies = []
+    waiting = []
+    low = 0
+    for i in range(PARTS):
         part = pl.ds(i * flux_width, flux_width)
-        copy = pltpu.make_async_copy(
-            flux_hbm.at[:, :, part], flux.at[:, :, part], flux_sem.at[i]
-        )
-        copy.start()
-        flux_copies.append(copy)
-    tile_copies = []
-    low = 0
-    for i, size in enumerate(chunks):
-        part = pl.ds(low, size)
-        low += size
-        tile_copies.append(
-            pltpu.make_async_copy(tiles_hbm.at[part], tiles.at[part], tile_sem.at[i])
-        )
-    waiting = list(tile_copies)
+        flux_copies.append(
+            pltpu.make_async_copy(flux_hbm.at[:, :, part], flux.at[:, :, part], flux_sem.at[i])
+        )
+        for size in copy_plan[i]:
+            part = pl.ds(low, size)
+            low += size
+            copy = pltpu.make_async_copy(
+                tiles_hbm.at[part], tiles.at[part], tile_sem.at[len(tile_copies)]
+            )
+            tile_copies.append((low, copy))
+            waiting.append(copy)
 
     def start_more(count):
         for copy in waiting[:count]:
-            copy.start()
+            copy.start(priority=1)
         del waiting[:count]
 
-    start_more(AHEAD)
+    flux_copies[0].start()
+    start_more(DEPTH)
+    flux_copies[1].start()
+    small[0].start()
 
     barrier = pltpu.get_barrier_semaphore()
     rivals = []
@@ -163,14 +171,7 @@
             lhs[:, pl.ds(base + 128, 128)] = right[:, cut]
         return total + value, area_total + a
 
-    carry = (jnp.zeros((fields, width), F32), jnp.zeros((1, width), F32))
-    rounds = flux_width // width
-    for i in range(FLUX_PARTS):
-        flux_copies[i].wait()
-        start_more(1)
-        carry = lax.fori_loop(i * rounds, (i + 1) * rounds, weigh, carry, unroll=rounds)
-    surface_num = jnp.sum(carry[0], axis=1, keepdims=True)
-    surface_den = jnp.sum(carry[1])
+    early = blocks - blocks // PARTS
 
     def pair(j, carry):
         left = lhs[:, pl.ds(pl.multiple_of(j * 256, 256), 256)]
@@ -182,11 +183,30 @@
         r = jnp.dot(left, jnp.concatenate(right, axis=1), preferred_element_type=F32)
         r = r[: 2 * fields] + r[2 * fields :]
         for t in range(slots):
-            base = pl.multiple_of((t * blocks + 2 * j) * fields, 2 * fields)
+            base = pl.multiple_of((t * carry[1] + carry[0] + 2 * j) * fields, 2 * fields)
             for q in range(lane_tiles):
                 n = t * lane_tiles + q
                 contrib[q, pl.ds(base, 2 * fields), :] = r[:, n * 128 : (n + 1) * 128]
         return carry
+
+    def select(low, count):
+        for t in range(slots):
+            picks[:, pl.ds(2 * low + t * count, count)] = targets[pl.ds(t, 1), pl.ds(low, count)]
+        tile_ids = picks[:, pl.ds(2 * low, slots * count)]
+        owner_ids = lax.broadcasted_iota(jnp.int32, (owners, slots * count), 0)
+        return jnp.where(owner_ids == tile_ids, 1.0, 0.0).astype(BF16)
+
+    def collect(low, count, selector, g):
+        right = []
+        for f in (2 * g, 2 * g + 1):
+            for q in range(lane_tiles):
+                rows = pl.ds(slots * low * fields + f, slots * count, stride=fields)
+                right.append(split(contrib[q, rows, :]))
+        his = jnp.concatenate([r[0] for r in right], axis=1)
+        los = jnp.concatenate([r[1] for r in right], axis=1)
+        s = jnp.dot(selector, his, preferred_element_type=F32)
+        s = s + jnp.dot(selector, los, preferred_element_type=F32)
+        return [s[:, n * air_cells : (n + 1) * air_cells] for n in range(2)]
 
     def row_copy(p, slot):
         return pltpu.make_async_remote_copy(
@@ -198,56 +218,66 @@
             device_id_type=MESH,
         )
 
+    totals = (jnp.zeros((fields, width), F32), jnp.zeros((1, width), F32))
+    weigh_rounds = flux_width // width
     low = 0
-    for i, size in enumerate(chunks):
-        if i == SEND_ROWS_AT:
-            small[0].wait()
-            for c in range(groups):
-                for q in range(lane_tiles):
-                    row = fraction[pl.ds(c, 1), pl.ds(q * 128, 128)]
-                    row_out[pl.ds(c * lane_tiles + q, 1), :] = row
-                    rows_in[pl.ds(dom * 8 + c * lane_tiles + q, 1), :] = row
-            pl.semaphore_wait(barrier, owners - 1)
-            for c, p in rivals:
-                row_copy(p, dom).start()
-        tile_copies[i].wait()
-        start_more(1)
-        if i == 3:
+    arrived = 0
+    step = 0
+    for i in range(PARTS):
+        flux_copies[i].wait()
+        if i + 2 < PARTS:
+            flux_copies[i + 2].start()
+        if i == 1:
             for copy in small[3:]:
                 copy.start()
-        pairs = size // 2
-        lax.fori_loop(low, low + pairs, pair, 0, unroll=min(UNROLL, pairs))
-        low += pairs
-
-    small[3].wait()
-    picks[:, pl.ds(0, blocks)] = targets[...]
-    picks[:, pl.ds(blocks, blocks)] = targets[...]
-    picked = jnp.where(
-        lax.broadcasted_iota(jnp.int32, (1, tile_count), 1) < blocks,
-        picks[pl.ds(0, 1), :],
-        picks[pl.ds(1, 1), :],
-    )
-    owner_ids = lax.broadcasted_iota(jnp.int32, (owners, tile_count), 0)
-    selector = jnp.where(owner_ids == picked, 1.0, 0.0).astype(BF16)
-    selector = jnp.concatenate([selector, selector], axis=1)
-
-    def collect(g, carry):
-        right = []
-        for f in (2 * g, 2 * g + 1):
-            for q in range(lane_tiles):
-                hi, lo = split(contrib[q, pl.ds(f, tile_count, stride=fields), :])
-                right.append(jnp.concatenate([hi, lo], axis=0))
-        s = jnp.dot(selector, jnp.concatenate(right, axis=1), preferred_element_type=F32)
-        for n, f in enumerate((2 * g, 2 * g + 1)):
-            summed[f] = s[:, n * air_cells : (n + 1) * air_cells]
-        return carry
+        totals = lax.fori_loop(
+            i * weigh_rounds, (i + 1) * weigh_rounds, weigh, totals, unroll=weigh_rounds
+        )
+        for size in round_plan[i]:
+            if step == SEND_ROWS_AT:
+                small[0].wait()
+                for c in range(groups):
+                    for q in range(lane_tiles):
+                        row = fraction[pl.ds(c, 1), pl.ds(q * 128, 128)]
+                        row_out[pl.ds(c * lane_tiles + q, 1), :] = row
+                        rows_in[pl.ds(dom * 8 + c * lane_tiles + q, 1), :] = row
+                start_more(EXTRA)
+                pl.semaphore_wait(barrier, owners - 1)
+                for c, p in rivals:
+                    row_copy(p, dom).start()
+            step += 1
+            while arrived < len(tile_copies) and tile_copies[arrived][0] <= low + size:
+                tile_copies[arrived][1].wait()
+                start_more(1)
+                arrived += 1
+            first_block, count = (0, early) if low < early else (early, blocks - early)
+            place = (slots * first_block - first_block, count)
+            pairs = size // 2
+            lax.fori_loop(
+                low // 2,
+                low // 2 + pairs,
+                lambda j, c, place=place: (pair(j, place), c)[1],
+                0,
+                unroll=min(UNROLL, pairs),
+            )
+            low += size
+        if low == early:
+            small[3].wait()
+            selector = select(0, early)
+            last_selector = select(early, blocks - early)
+            for g in range(fields // 2):
+                summed[2 * g], summed[2 * g + 1] = collect(0, early, selector, g)
 
     far = pl.ds(pl.multiple_of(other * domains, 8), domains)
     own = pl.ds(pl.multiple_of(comp * domains, 8), domains)
     per_cut = fields // PAIR_CUTS
     pair_copies = []
+    last = []
+    for g in range(fields // 2):
+        last.extend(collect(early, blocks - early, last_selector, g))
     for n in range(PAIR_CUTS):
-        lax.fori_loop(n * per_cut // 2, (n + 1) * per_cut // 2, collect, 0, unroll=per_cut // 2)
+        for f in range(n * per_cut, (n + 1) * per_cut):
+            summed[f] = summed[f] + last[f]
         part = pl.ds(n * per_cut, per_cut)
         copy = pltpu.make_async_remote_copy(
             src_ref=summed.at[part, far],
@@ -260,6 +290,8 @@
         copy.start()
         pair_copies.append(copy)
 
+    surface_num = jnp.sum(totals[0], axis=1, keepdims=True)
+    surface_den = jnp.sum(totals[1])
     small[4].wait()
     small[5].wait()
     air_row = air[...].reshape(1, air_cells)
@@ -297,15 +329,38 @@
     share_own = shares(comp)
     share_other = shares(other)
 
-    def main_copy(p, slot):
+    half = domains // 2
+    side = dom // half
+    seat = dom % half
+    bit = 1 + comp
+    flip = dom // bit % 2
+    neighbour = dom + bit * (1 - 2 * flip)
+
+    def across(m, value):
+        one = 2 * m + value
+        two = m // 2 * 4 + 2 * value + m % 2
+        return (1 - side) * half + one + comp * (two - one)
+
+    rank = seat // 2 + comp * (seat // 4 * 2 + seat % 2 - seat // 2)
+    mates_here = [side * half + k + jnp.where(seat <= k, 1, 0) for k in range(half - 1)]
+
+    def message(src, dst, p, sem):
         return pltpu.make_async_remote_copy(
-            src_ref=outgoing.at[p, pl.ds(0, body_rows + 1)],
-            dst_ref=incoming.at[slot, pl.ds(0, body_rows + 1)],
+            src_ref=src.at[pl.ds(0, body_rows + 1)],
+            dst_ref=dst.at[pl.ds(0, body_rows + 1)],
             send_sem=main_send,
-            recv_sem=main_recv.at[slot],
+            recv_sem=main_recv.at[sem],
             device_id=(comp, p),
             device_id_type=MESH,
         )
+
+    def relay_copy(m):
+        return message(
+            outgoing.at[across(m, 1 - flip)], relayed.at[m], neighbour, domains + m
+        )
+
+    def direct_copy(p, slot):
+        return message(outgoing.at[p], incoming.at[slot], p, slot)
 
     def stat_copy(p, slot):
         return pltpu.make_async_remote_copy(
@@ -333,19 +388,40 @@
     stat = stat + jnp.sum(air_num, axis=0, keepdims=True)
     outgoing[:, body_rows, :] = jnp.broadcast_to(stat, (domains, 128))
     stat_out[...] = stat
+    for m in range(AT_ONCE):
+        for value in range(2):
+            group = jnp.where(flip == value, 0, half // 2)
+            direct_copy(across(m, value), half + rank + group).start()
+    for m in range(AT_ONCE, half // 2):
+        relay_copy(m).start()
     for k in range(domains):
         stat_copy(k, dom).start()
-    for c, p in rivals:
-        main_copy(p, dom).start()
-
+    for m in range(AT_ONCE, half // 2):
+        if m == SIDE_AT:
+            for p in mates_here:
+                direct_copy(p, seat).start()
+        relay_copy(m).wait_recv()
+        p = across(m, flip)
+        outgoing[p] = outgoing[p] + relayed[m]
+        direct_copy(p, half + rank).start()
+
+    @pl.when(rank < AT_ONCE)
+    def _():
+        for m in range(half // 2):
+            slot = half + half // 2 + m
+            direct_copy(dom, slot).wait_recv()
+            outgoing[dom] = outgoing[dom] + incoming[slot]
+
+    stat = outgoing[dom, pl.ds(body_rows, 1), :]
     sums = []
     for q in range(lane_tiles):
         sums.append(outgoing[dom, pl.ds(q * fields, fields), :])
-    for c, p in rivals:
-        main_copy(p, p).wait_recv()
+    slots_in = [p % half for p in mates_here] + [half + m for m in range(half // 2)]
+    for slot in slots_in:
+        direct_copy(dom, slot).wait_recv()
         for q in range(lane_tiles):
-            sums[q] = sums[q] + incoming[p, pl.ds(q * fields, fields), :]
-        stat = stat + incoming[p, pl.ds(body_rows, 1), :]
+            sums[q] = sums[q] + incoming[slot, pl.ds(q * fields, fields), :]
+        stat = stat + incoming[slot, pl.ds(body_rows, 1), :]
     for q in range(lane_tiles):
         cut = slice(q * 128, (q + 1) * 128)
         merged_ref[:, cut] = sums[q] * inverse[:, cut] + ocean_part[:, cut]
@@ -438,7 +514,7 @@
             pltpu.VMEM((2 * fields, cells), F32),
             pltpu.VMEM((4 * fields, 2 * cells), BF16),
             pltpu.VMEM((lane_tiles, blocks * slots * fields, 128), F32),
-            pltpu.VMEM((slots, blocks * slots), jnp.int32),
+            pltpu.VMEM((1, blocks * slots), jnp.int32),
             pltpu.VMEM((groups * lane_tiles, 128), F32),
             pltpu.VMEM((domains * 8, 128), F32),
             pltpu.VMEM((fields, owners, air_cells), F32),
@@ -448,8 +524,9 @@
             pltpu.VMEM((domains, 1, 128), F32),
             pltpu.VMEM((domains, message, 128), F32),
             pltpu.VMEM((domains, message, 128), F32),
-            dma((FLUX_PARTS,)),
-            dma((len(chunk_sizes(blocks)),)),
+            pltpu.VMEM((domains // 4, message, 128), F32),
+            dma((PARTS,)),
+            dma((sum(len(c) for c in plan(blocks)[0]),)),
             dma((6,)),
             dma,
             dma,
@@ -458,7 +535,7 @@
             dma,
             dma,
             dma,
-            dma((domains,)),
+            dma((domains + domains // 4,)),
         ],
         compiler_params=pltpu.CompilerParams(
             collective_id=0, has_side_effects=True, vmem_limit_bytes=60 * 1024 * 1024

time: 21 us -> 19.9 us (0.948)
  Pallas kernels: 20.2 us -> 19.1 us
    pallas_call x1, Pallas kernels: 19.6 us -> 18.5 us  [on_device(): pl.pallas_call(functools.partial(kernel, groups, domains), out_shape=(plt...]
where the time goes in v2:
time: 19.9 us; the launch traced here: 19.7 us
  Pallas kernels  19.1 us (96%)
  between operations  0.64 us (3%)
    pallas_call x1, Pallas kernels, on_device(): pl.pallas_call(functools.partial(kernel, groups, domains), out_shape=(plt...  18.5 us
    pallas_call x1, Pallas kernels, on_device(): pl.pallas_call(finish, out_shape=(jax.ShapeDtypeStruct((fields, air_cells...  0.61 us

profile of v2, /device:TPU:0, one launch (start us, length us, event | category | flops | bytes accessed | tf_op | source)
XLA Modules:
  0.0 19.7 jit_solution(15109666956749402665)
XLA Ops:
  0.6 18.5 %shard_map.95 = (f32[12,384]{1,0:T(8,128)S(1)}, f32[3,12]{1,0:T(4,128)S(1)}) custom-call(f32[6,12,4096]{2,1,0:T(8,128)} %flux_hbm.1, s32[1,4096]{1,0:T(1,128)} %bitcast.3, f32[1,4096]{1,0:T(1,128)} %bitcast.4, s32[2,64]{1,0:T(2,128)} %bitcast.5, f32[64,2,64,384]{3,2,1,0:T(8,128)} %tiles_hbm.1, f32[12,384]{1,0:T(8,128)} %ocean_hbm.1, f32[3,384]{1,0:T(4,128)} %fraction_hbm.1, ...), custom_call_target="tpu_custom_call" | custom-call | tf_op jit(solution)/shard_map/pallas_call | solution.py:497
  19.1 0.6 %shard_map.96 = (f32[12,384]{1,0:T(8,128)}, f32[3,12]{1,0:T(4,128)}) custom-call(f32[12,384]{1,0:T(8,128)S(1)} %get-tuple-element.4.merged_in, f32[3,12]{1,0:T(4,128)S(1)} %get-tuple-element.5.means_in), custom_call_target="tpu_custom_call" | custom-call | tf_op jit(solution)/shard_map/pallas_call | solution.py:553

commit v3 on v2

--- a/solution.py
+++ b/solution.py
@@ -10,14 +10,13 @@
 MESH = pl.DeviceIdType.MESH
 F32 = jnp.float32
 BF16 = jnp.bfloat16
-DEPTH = 8
+DEPTH = 12
 EXTRA = 4
-SEND_ROWS_AT = 2
+TURNS = (1, 2, 3)
 PARTS = 4
 UNROLL = 8
 PAIR_CUTS = 3
-AT_ONCE = 1
-SIDE_AT = 1
+SIDE_AT = 3
 
 
 def split(x):
@@ -129,9 +128,9 @@
             copy.start(priority=1)
         del waiting[:count]
 
-    flux_copies[0].start()
+    for copy in flux_copies:
+        copy.start()
     start_more(DEPTH)
-    flux_copies[1].start()
     small[0].start()
 
     barrier = pltpu.get_barrier_semaphore()
@@ -218,6 +217,24 @@
             device_id_type=MESH,
         )
 
+    def send_rows():
+        small[0].wait()
+        for c in range(groups):
+            for q in range(lane_tiles):
+                row = fraction[pl.ds(c, 1), pl.ds(q * 128, 128)]
+                row_out[pl.ds(c * lane_tiles + q, 1), :] = row
+                rows_in[pl.ds(dom * 8 + c * lane_tiles + q, 1), :] = row
+        pl.semaphore_wait(barrier, owners - 1)
+        for c, p in rivals:
+            row_copy(p, dom).start()
+
+    quarter = domains // 4
+    turns = [
+        (TURNS[0], (3 * quarter, domains)),
+        (TURNS[1], (2 * quarter, 3 * quarter)),
+        (TURNS[2], (1, 2 * quarter)),
+    ]
+
     totals = (jnp.zeros((fields, width), F32), jnp.zeros((1, width), F32))
     weigh_rounds = flux_width // width
     low = 0
@@ -225,8 +242,6 @@
     step = 0
     for i in range(PARTS):
         flux_copies[i].wait()
-        if i + 2 < PARTS:
-            flux_copies[i + 2].start()
         if i == 1:
             for copy in small[3:]:
                 copy.start()
@@ -234,17 +249,8 @@
             i * weigh_rounds, (i + 1) * weigh_rounds, weigh, totals, unroll=weigh_rounds
         )
         for size in round_plan[i]:
-            if step == SEND_ROWS_AT:
-                small[0].wait()
-                for c in range(groups):
-                    for q in range(lane_tiles):
-                        row = fraction[pl.ds(c, 1), pl.ds(q * 128, 128)]
-                        row_out[pl.ds(c * lane_tiles + q, 1), :] = row
-                        rows_in[pl.ds(dom * 8 + c * lane_tiles + q, 1), :] = row
-                start_more(EXTRA)
-                pl.semaphore_wait(barrier, owners - 1)
-                for c, p in rivals:
-                    row_copy(p, dom).start()
+            for low_dom, high_dom in [span for at, span in turns if at == step]:
+                pl.when((dom >= low_dom) & (dom < high_dom))(send_rows)
             step += 1
             while arrived < len(tile_copies) and tile_copies[arrived][0] <= low + size:
                 tile_copies[arrived][1].wait()
@@ -268,6 +274,8 @@
             for g in range(fields // 2):
                 summed[2 * g], summed[2 * g + 1] = collect(0, early, selector, g)
 
+    pl.when(dom == 0)(send_rows)
+
     far = pl.ds(pl.multiple_of(other * domains, 8), domains)
     own = pl.ds(pl.multiple_of(comp * domains, 8), domains)
     per_cut = fields // PAIR_CUTS
@@ -388,27 +396,40 @@
     stat = stat + jnp.sum(air_num, axis=0, keepdims=True)
     outgoing[:, body_rows, :] = jnp.broadcast_to(stat, (domains, 128))
     stat_out[...] = stat
-    for m in range(AT_ONCE):
-        for value in range(2):
-            group = jnp.where(flip == value, 0, half // 2)
-            direct_copy(across(m, value), half + rank + group).start()
-    for m in range(AT_ONCE, half // 2):
-        relay_copy(m).start()
+    def at_once(target):
+        return (dom >= 2 * quarter) & (target == 0)
+
+    for m in range(half // 2):
+        target = across(m, 1 - flip)
+
+        @pl.when(at_once(target))
+        def _(target=target):
+            direct_copy(target, domains - half // 2 + rank).start()
+
+        @pl.when(jnp.logical_not(at_once(target)))
+        def _(m=m):
+            relay_copy(m).start()
+
+    direct_copy(mates_here[0], seat).start()
     for k in range(domains):
         stat_copy(k, dom).start()
-    for m in range(AT_ONCE, half // 2):
+    for m in range(half // 2):
         if m == SIDE_AT:
-            for p in mates_here:
+            for p in mates_here[1:]:
                 direct_copy(p, seat).start()
-        relay_copy(m).wait_recv()
-        p = across(m, flip)
-        outgoing[p] = outgoing[p] + relayed[m]
-        direct_copy(p, half + rank).start()
-
-    @pl.when(rank < AT_ONCE)
+        target = across(m, flip)
+
+        @pl.when(jnp.logical_not(at_once(target)))
+        def _(m=m, target=target):
+            relay_copy(m).wait_recv()
+            outgoing[target] = outgoing[target] + relayed[m]
+
+        direct_copy(target, half + rank).start()
+
+    @pl.when(dom == 0)
     def _():
         for m in range(half // 2):
-            slot = half + half // 2 + m
+            slot = domains - half // 2 + m
             direct_copy(dom, slot).wait_recv()
             outgoing[dom] = outgoing[dom] + incoming[slot]
 

time: 19.9 us -> 19.1 us (0.960)
  Pallas kernels: 19.1 us -> 18.1 us
    pallas_call x1, Pallas kernels: 18.5 us -> 17.5 us  [on_device(): pl.pallas_call(functools.partial(kernel, groups, domains), out_shape=(plt...]
where the time goes in v3:
time: 19.1 us; the launch traced here: 18.8 us
  Pallas kernels  18.1 us (95%)
  between operations  0.64 us (3%)
    pallas_call x1, Pallas kernels, on_device(): pl.pallas_call(functools.partial(kernel, groups, domains), out_shape=(plt...  17.5 us
    pallas_call x1, Pallas kernels, on_device(): pl.pallas_call(finish, out_shape=(jax.ShapeDtypeStruct((fields, air_cells...  0.61 us

profile of v3, /device:TPU:0, one launch (start us, length us, event | category | flops | bytes accessed | tf_op | source)
XLA Modules:
  0.0 18.8 jit_solution(11921695046439953388)
XLA Ops:
  0.6 17.5 %shard_map.95 = (f32[12,384]{1,0:T(8,128)S(1)}, f32[3,12]{1,0:T(4,128)S(1)}) custom-call(f32[6,12,4096]{2,1,0:T(8,128)} %flux_hbm.1, s32[1,4096]{1,0:T(1,128)} %bitcast.3, f32[1,4096]{1,0:T(1,128)} %bitcast.4, s32[2,64]{1,0:T(2,128)} %bitcast.5, f32[64,2,64,384]{3,2,1,0:T(8,128)} %tiles_hbm.1, f32[12,384]{1,0:T(8,128)} %ocean_hbm.1, f32[3,384]{1,0:T(4,128)} %fraction_hbm.1, ...), custom_call_target="tpu_custom_call" | custom-call | tf_op jit(solution)/shard_map/pallas_call | solution.py:518
  18.1 0.6 %shard_map.96 = (f32[12,384]{1,0:T(8,128)}, f32[3,12]{1,0:T(4,128)}) custom-call(f32[12,384]{1,0:T(8,128)S(1)} %get-tuple-element.4.merged_in, f32[3,12]{1,0:T(4,128)S(1)} %get-tuple-element.5.means_in), custom_call_target="tpu_custom_call" | custom-call | tf_op jit(solution)/shard_map/pallas_call | solution.py:574

commit v4 on v3

--- a/solution.py
+++ b/solution.py
@@ -10,13 +10,12 @@
 MESH = pl.DeviceIdType.MESH
 F32 = jnp.float32
 BF16 = jnp.bfloat16
-DEPTH = 12
-EXTRA = 4
+DEPTH = 5
 TURNS = (1, 2, 3)
 PARTS = 4
 UNROLL = 8
 PAIR_CUTS = 3
-SIDE_AT = 3
+SIDE_AT = (0, 99)
 
 
 def split(x):
@@ -27,9 +26,8 @@
 
 def plan(blocks):
     whole = blocks // PARTS
-    copies = [[whole // 4] * 4] * PARTS
     rounds = [[whole // 2] * 2] + [[whole]] * (PARTS - 2) + [[whole // 2, whole // 4, whole // 4]]
-    return copies, rounds
+    return rounds, rounds
 
 
 def kernel(
@@ -91,14 +89,14 @@
 
     small = [
         pltpu.make_async_copy(src, dst, small_sem.at[i])
-        for i, (src, dst) in enumerate(
+        for i, src, dst in (
             [
-                (fraction_hbm, fraction),
-                (mask_hbm, mask),
-                (area_hbm, area),
-                (targets_hbm, targets),
-                (ocean_hbm, ocean),
-                (air_hbm, air),
+                (0, fraction_hbm, fraction),
+                (1, mask_hbm, mask),
+                (1, area_hbm, area),
+                (2, targets_hbm, targets),
+                (3, ocean_hbm, ocean),
+                (4, air_hbm, air),
             ]
         )
     ]
@@ -143,8 +141,8 @@
             if peer is not None:
                 pl.semaphore_signal(barrier, inc=1, device_id=peer, device_id_type=MESH)
 
-    small[1].wait()
-    small[2].wait()
+    both_rows = contrib.at[0, pl.ds(0, 2 * cells // 128)]
+    pltpu.make_async_copy(both_rows, both_rows, small_sem.at[1]).wait()
     width = min(512, flux_width)
     lane = lax.broadcasted_iota(jnp.int32, (fields, width), 1)
     first = lax.rem(lane, 2 * block_cells) < block_cells
@@ -290,7 +288,7 @@
         copy = pltpu.make_async_remote_copy(
             src_ref=summed.at[part, far],
             dst_ref=partner_in.at[part],
-            send_sem=pair_send.at[n],
+            send_sem=pair_send,
             recv_sem=pair_recv.at[n],
             device_id=(other, dom),
             device_id_type=MESH,
@@ -364,11 +362,22 @@
 
     def relay_copy(m):
         return message(
-            outgoing.at[across(m, 1 - flip)], relayed.at[m], neighbour, domains + m
-        )
-
-    def direct_copy(p, slot):
-        return message(outgoing.at[p], incoming.at[slot], p, slot)
+            outgoing.at[across(m, 1 - flip)], relayed.at[m], neighbour, 3 + m
+        )
+
+    def direct_copy(p, kind, slot):
+        return message(outgoing.at[p], incoming.at[slot], p, kind)
+
+    def wait_all(kind, count):
+        block = incoming.at[pl.ds(0, count), pl.ds(0, body_rows + 1)]
+        pltpu.make_async_remote_copy(
+            src_ref=block,
+            dst_ref=block,
+            send_sem=main_send,
+            recv_sem=main_recv.at[kind],
+            device_id=(other, dom),
+            device_id_type=MESH,
+        ).wait_recv()
 
     def stat_copy(p, slot):
         return pltpu.make_async_remote_copy(
@@ -399,24 +408,28 @@
     def at_once(target):
         return (dom >= 2 * quarter) & (target == 0)
 
+    def send_side():
+        for p in mates_here[1:]:
+            direct_copy(p, 0, seat).start()
+
     for m in range(half // 2):
         target = across(m, 1 - flip)
 
         @pl.when(at_once(target))
         def _(target=target):
-            direct_copy(target, domains - half // 2 + rank).start()
+            direct_copy(target, 2, domains - half // 2 + rank).start()
 
         @pl.when(jnp.logical_not(at_once(target)))
         def _(m=m):
             relay_copy(m).start()
 
-    direct_copy(mates_here[0], seat).start()
+    direct_copy(mates_here[0], 0, seat).start()
     for k in range(domains):
         stat_copy(k, dom).start()
     for m in range(half // 2):
-        if m == SIDE_AT:
-            for p in mates_here[1:]:
-                direct_copy(p, seat).start()
+        for at, where in zip(SIDE_AT, range(2)):
+            if m == at:
+                pl.when(side == where)(send_side)
         target = across(m, flip)
 
         @pl.when(jnp.logical_not(at_once(target)))
@@ -424,25 +437,31 @@
             relay_copy(m).wait_recv()
             outgoing[target] = outgoing[target] + relayed[m]
 
-        direct_copy(target, half + rank).start()
+        direct_copy(target, 1, half + rank).start()
+    pl.when(side == 1)(send_side)
+
+    def gathered(slots_in):
+        body = [
+            sum(incoming[slot, pl.ds(q * fields, fields), :] for slot in slots_in)
+            for q in range(lane_tiles)
+        ]
+        return body, sum(incoming[slot, pl.ds(body_rows, 1), :] for slot in slots_in)
+
+    wait_all(0, half - 1)
+    sums, stat = gathered([p % half for p in mates_here])
 
     @pl.when(dom == 0)
     def _():
+        wait_all(2, half // 2)
         for m in range(half // 2):
-            slot = domains - half // 2 + m
-            direct_copy(dom, slot).wait_recv()
-            outgoing[dom] = outgoing[dom] + incoming[slot]
-
-    stat = outgoing[dom, pl.ds(body_rows, 1), :]
-    sums = []
-    for q in range(lane_tiles):
-        sums.append(outgoing[dom, pl.ds(q * fields, fields), :])
-    slots_in = [p % half for p in mates_here] + [half + m for m in range(half // 2)]
-    for slot in slots_in:
-        direct_copy(dom, slot).wait_recv()
-        for q in range(lane_tiles):
-            sums[q] = sums[q] + incoming[slot, pl.ds(q * fields, fields), :]
-        stat = stat + incoming[slot, pl.ds(body_rows, 1), :]
+            outgoing[dom] = outgoing[dom] + incoming[domains - half // 2 + m]
+
+    sums = [s + outgoing[dom, pl.ds(q * fields, fields), :] for q, s in enumerate(sums)]
+    stat = stat + outgoing[dom, pl.ds(body_rows, 1), :]
+    wait_all(1, half // 2)
+    late, late_stat = gathered(range(half, half + half // 2))
+    sums = [a + b for a, b in zip(sums, late)]
+    stat = stat + late_stat
     for q in range(lane_tiles):
         cut = slice(q * 128, (q + 1) * 128)
         merged_ref[:, cut] = sums[q] * inverse[:, cut] + ocean_part[:, cut]
@@ -469,8 +488,14 @@
         device_id=(other, dom),
         device_id_type=MESH,
     ).wait_send()
-    for copy in pair_copies:
-        copy.wait_send()
+    pltpu.make_async_remote_copy(
+        src_ref=partner_in,
+        dst_ref=partner_in,
+        send_sem=pair_send,
+        recv_sem=pair_recv.at[0],
+        device_id=(other, dom),
+        device_id_type=MESH,
+    ).wait_send()
     pltpu.make_async_remote_copy(
         src_ref=stat_in,
         dst_ref=stat_in,
@@ -489,9 +514,15 @@
     ).wait_send()
 
 
-def finish(merged_in, means_in, merged_ref, means_ref):
-    merged_ref[...] = merged_in[...]
-    means_ref[...] = means_in[...]
+def finish(merged_in, means_in, merged_hbm, means_hbm, sem):
+    copies = [
+        pltpu.make_async_copy(merged_in, merged_hbm, sem.at[0]),
+        pltpu.make_async_copy(means_in, means_hbm, sem.at[1]),
+    ]
+    for copy in copies:
+        copy.start()
+    for copy in copies:
+        copy.wait()
 
 
 def on_device(
@@ -548,15 +579,15 @@
             pltpu.VMEM((domains // 4, message, 128), F32),
             dma((PARTS,)),
             dma((sum(len(c) for c in plan(blocks)[0]),)),
-            dma((6,)),
+            dma((5,)),
             dma,
             dma,
-            dma((PAIR_CUTS,)),
+            dma,
             dma((PAIR_CUTS,)),
             dma,
             dma,
             dma,
-            dma((domains + domains // 4,)),
+            dma((3 + domains // 4,)),
         ],
         compiler_params=pltpu.CompilerParams(
             collective_id=0, has_side_effects=True, vmem_limit_bytes=60 * 1024 * 1024
@@ -578,7 +609,8 @@
             jax.ShapeDtypeStruct((groups + 1, fields), F32),
         ),
         in_specs=[vmem, vmem],
-        out_specs=(vmem, vmem),
+        out_specs=(hbm, hbm),
+        scratch_shapes=[dma((2,))],
     )(*[pltpu.with_memory_space_constraint(p, pltpu.VMEM) for p in parts])
 
 

time: 19.1 us -> 18.8 us (0.984)
  no operation moved by 1% of the time
where the time goes in v4:
time: 18.8 us; the launch traced here: 18.6 us
  Pallas kernels  18 us (96%)
  between operations  0.64 us (3%)
    pallas_call x1, Pallas kernels, on_device(): pl.pallas_call(functools.partial(kernel, groups, domains), out_shape=(plt...  17.3 us
    pallas_call x1, Pallas kernels, on_device(): pl.pallas_call(finish, out_shape=(jax.ShapeDtypeStruct((fields, air_cells...  0.63 us

profile of v4, /device:TPU:0, one launch (start us, length us, event | category | flops | bytes accessed | tf_op | source)
XLA Modules:
  0.0 18.6 jit_solution(2262993941528511894)
XLA Ops:
  0.6 17.3 %shard_map.95 = (f32[12,384]{1,0:T(8,128)S(1)}, f32[3,12]{1,0:T(4,128)S(1)}) custom-call(f32[6,12,4096]{2,1,0:T(8,128)} %flux_hbm.1, s32[1,4096]{1,0:T(1,128)} %bitcast.3, f32[1,4096]{1,0:T(1,128)} %bitcast.4, s32[2,64]{1,0:T(2,128)} %bitcast.5, f32[64,2,64,384]{3,2,1,0:T(8,128)} %tiles_hbm.1, f32[12,384]{1,0:T(8,128)} %ocean_hbm.1, f32[3,384]{1,0:T(4,128)} %fraction_hbm.1, ...), custom_call_target="tpu_custom_call" | custom-call | tf_op jit(solution)/shard_map/pallas_call | solution.py:549
  18.0 0.6 %shard_map.96 = (f32[12,384]{1,0:T(8,128)}, f32[3,12]{1,0:T(4,128)}) custom-call(f32[12,384]{1,0:T(8,128)S(1)} %get-tuple-element.4.merged_in, f32[3,12]{1,0:T(4,128)S(1)} %get-tuple-element.5.means_in), custom_call_target="tpu_custom_call" | custom-call | tf_op jit(solution)/shard_map/pallas_call | solution.py:605

commit v5 on v4

--- a/solution.py
+++ b/solution.py
@@ -458,14 +458,6 @@
 
     sums = [s + outgoing[dom, pl.ds(q * fields, fields), :] for q, s in enumerate(sums)]
     stat = stat + outgoing[dom, pl.ds(body_rows, 1), :]
-    wait_all(1, half // 2)
-    late, late_stat = gathered(range(half, half + half // 2))
-    sums = [a + b for a, b in zip(sums, late)]
-    stat = stat + late_stat
-    for q in range(lane_tiles):
-        cut = slice(q * 128, (q + 1) * 128)
-        merged_ref[:, cut] = sums[q] * inverse[:, cut] + ocean_part[:, cut]
-
     pltpu.make_async_remote_copy(
         src_ref=stat_in,
         dst_ref=stat_in,
@@ -475,6 +467,14 @@
         device_id_type=MESH,
     ).wait_recv()
     stat = stat + jnp.sum(stat_in[...], axis=0)
+    wait_all(1, half // 2)
+    late, late_stat = gathered(range(half, half + half // 2))
+    sums = [a + b for a, b in zip(sums, late)]
+    stat = stat + late_stat
+    for q in range(lane_tiles):
+        cut = slice(q * 128, (q + 1) * 128)
+        merged_ref[:, cut] = sums[q] * inverse[:, cut] + ocean_part[:, cut]
+
     mean = stat / pltpu.roll(stat, 64, 1)
     for c in range(groups + 1):
         moved = mean if c == 0 else pltpu.roll(mean, 128 - 16 * c, 1)

time: 18.8 us -> 18.8 us (level)
  no operation moved by 1% of the time
where the time goes in v5:
time: 18.8 us; the launch traced here: 18.6 us
  Pallas kernels  18 us (96%)
  between operations  0.64 us (3%)
    pallas_call x1, Pallas kernels, on_device(): pl.pallas_call(functools.partial(kernel, groups, domains), out_shape=(plt...  17.3 us
    pallas_call x1, Pallas kernels, on_device(): pl.pallas_call(finish, out_shape=(jax.ShapeDtypeStruct((fields, air_cells...  0.63 us

profile of v5, /device:TPU:0, one launch (start us, length us, event | category | flops | bytes accessed | tf_op | source)
XLA Modules:
  0.0 18.6 jit_solution(12048694771373907028)
XLA Ops:
  0.6 17.3 %shard_map.95 = (f32[12,384]{1,0:T(8,128)S(1)}, f32[3,12]{1,0:T(4,128)S(1)}) custom-call(f32[6,12,4096]{2,1,0:T(8,128)} %flux_hbm.1, s32[1,4096]{1,0:T(1,128)} %bitcast.3, f32[1,4096]{1,0:T(1,128)} %bitcast.4, s32[2,64]{1,0:T(2,128)} %bitcast.5, f32[64,2,64,384]{3,2,1,0:T(8,128)} %tiles_hbm.1, f32[12,384]{1,0:T(8,128)} %ocean_hbm.1, f32[3,384]{1,0:T(4,128)} %fraction_hbm.1, ...), custom_call_target="tpu_custom_call" | custom-call | tf_op jit(solution)/shard_map/pallas_call | solution.py:549
  18.0 0.6 %shard_map.96 = (f32[12,384]{1,0:T(8,128)}, f32[3,12]{1,0:T(4,128)}) custom-call(f32[12,384]{1,0:T(8,128)S(1)} %get-tuple-element.4.merged_in, f32[3,12]{1,0:T(4,128)S(1)} %get-tuple-element.5.means_in), custom_call_target="tpu_custom_call" | custom-call | tf_op jit(solution)/shard_map/pallas_call | solution.py:605

commit v6 on v5

--- a/solution.py
+++ b/solution.py
@@ -26,7 +26,7 @@
 
 def plan(blocks):
     whole = blocks // PARTS
-    rounds = [[whole // 2] * 2] + [[whole]] * (PARTS - 2) + [[whole // 2, whole // 4, whole // 4]]
+    rounds = [[whole // 2] * 2] + [[whole]] * (PARTS - 2) + [[whole // 2, whole // 2]]
     return rounds, rounds
 
 

time: 18.8 us -> 18.7 us (level)
  Pallas kernels: 18 us -> 17.8 us
where the time goes in v6:
time: 18.7 us; the launch traced here: 18.5 us
  Pallas kernels  17.8 us (95%)
  between operations  0.64 us (3%)
    pallas_call x1, Pallas kernels, on_device(): pl.pallas_call(functools.partial(kernel, groups, domains), out_shape=(plt...  17.2 us
    pallas_call x1, Pallas kernels, on_device(): pl.pallas_call(finish, out_shape=(jax.ShapeDtypeStruct((fields, air_cells...  0.63 us

profile of v6, /device:TPU:0, one launch (start us, length us, event | category | flops | bytes accessed | tf_op | source)
XLA Modules:
  0.0 18.5 jit_solution(9148103504429717218)
XLA Ops:
  0.6 17.2 %shard_map.95 = (f32[12,384]{1,0:T(8,128)S(1)}, f32[3,12]{1,0:T(4,128)S(1)}) custom-call(f32[6,12,4096]{2,1,0:T(8,128)} %flux_hbm.1, s32[1,4096]{1,0:T(1,128)} %bitcast.3, f32[1,4096]{1,0:T(1,128)} %bitcast.4, s32[2,64]{1,0:T(2,128)} %bitcast.5, f32[64,2,64,384]{3,2,1,0:T(8,128)} %tiles_hbm.1, f32[12,384]{1,0:T(8,128)} %ocean_hbm.1, f32[3,384]{1,0:T(4,128)} %fraction_hbm.1, ...), custom_call_target="tpu_custom_call" | custom-call | tf_op jit(solution)/shard_map/pallas_call | solution.py:549
  17.9 0.6 %shard_map.96 = (f32[12,384]{1,0:T(8,128)}, f32[3,12]{1,0:T(4,128)}) custom-call(f32[12,384]{1,0:T(8,128)S(1)} %get-tuple-element.4.merged_in, f32[3,12]{1,0:T(4,128)S(1)} %get-tuple-element.5.means_in), custom_call_target="tpu_custom_call" | custom-call | tf_op jit(solution)/shard_map/pallas_call | solution.py:605
